TPU v7x, 32 devices: a whole 2x2x4 slice. The times are simulated.
32 devices in a mesh: rows: 8 (over y, x, core), dim: 4 (over z).
Axes of the slice: x: 2, y: 2, z: 4, core: 2. Of those that a mesh axis runs over, the one named last changes fastest.
Arguments:
- entity_table: float32 [131072, 512], P(('rows', 'dim')), may hold values from -2.5 to 2.5
- relations: float32 [822, 512], replicated, may hold values from -6 to 6
- thresholds: float32 [64], replicated, may hold values from 0.2 to 2
- head_ids: int32 [2048], replicated, may hold values from 0 to 131071
- rel_ids: int32 [2048], replicated, may hold values from 0 to 821
- thr_idx: int32 [2048], replicated, may hold values from 0 to 63
Outputs:
- serving_table: float32 [131072, 512], P('rows', 'dim')
- fraction: float32 [2048], P(('rows', 'dim'))
All inputs are finite; a program needn't handle non-finite values.
Results may differ from a plain program's by a relative error of at most 0.0011.
Values sent between devices are 32-bit elements; how exact they have to be, the bound alone decides.
A program may use at most 128 MiB of HBM per device.

v0:
```python
import jax
import jax.numpy as jnp
from jax import lax
from jax.sharding import PartitionSpec as P

sharpness = 2.0


def pick_rows(table, head_ids, start):
    count = table.shape[0]
    local = head_ids - start
    owned = (local >= 0) & (local < count)
    picked = jnp.take(table, jnp.clip(local, 0, count - 1), axis=0)
    return jnp.where(owned[:, None], picked, jnp.zeros_like(picked))


def shards(entity_table, relations, thresholds, head_ids, rel_ids, thr_idx):
    local_rows = entity_table.shape[0]
    width = entity_table.shape[1]
    total_ents = local_rows * lax.axis_size("rows") * lax.axis_size("dim")
    serving = lax.all_to_all(entity_table, "dim", split_axis=1, concat_axis=0, tiled=True)
    start = (lax.axis_index("rows") * lax.axis_size("dim") + lax.axis_index("dim")) * local_rows
    partial_value = pick_rows(entity_table, head_ids, start)
    head_vecs = lax.psum(partial_value, ("rows", "dim"))
    query = (head_vecs * jnp.take(relations, rel_ids, axis=0)).astype(jnp.bfloat16)
    ent_low = entity_table.astype(jnp.bfloat16)
    level = jnp.take(thresholds, thr_idx)
    queries = query.shape[0]
    query_blocks = query.reshape(queries // 512, 512, width)
    level_blocks = level.reshape(queries // 512, 512)

    def score_block(pair):
        rows_q, rows_level = pair
        score = jnp.dot(rows_q, ent_low.T, preferred_element_type=jnp.float32)
        soft = jax.nn.sigmoid(sharpness * (score - rows_level[:, None]))
        return jnp.sum(soft, axis=1) * (1.0 / total_ents)

    partial_share = lax.map(score_block, (query_blocks, level_blocks)).reshape(queries)
    fraction = lax.psum_scatter(partial_share, ("rows", "dim"), scatter_dimension=0, tiled=True)
    return (serving, fraction)


def solution(mesh):
    placed = (P(("rows", "dim"), None), P(), P(), P(), P(), P())
    return jax.shard_map(
        shards,
        mesh=mesh,
        in_specs=placed,
        out_specs=(P("rows", "dim"), P(("rows", "dim"))),
        check_vma=False,
    )
```

profile of v0, /device:TPU:0, one launch (start us, length us, event | category | flops | bytes accessed | tf_op | source)
XLA Modules:
  0.0 399.6 jit_solution(839341070260288952)
XLA Ops:
  7.2 7.4 %copy_bitcast_fusion = f32[4096,4,128]{2,0,1:T(8,128)} fusion(f32[4096,512]{1,0:T(8,128)} %param.8), kind=kLoop, calls=%fused_computation.9 | loop fusion | bytes 16777216 | tf_op jit(solution)/shard_map/all_to_all | solution.py:21
  14.6 6.5 %all-to-all-start = ((f32[4096,4,128]{2,0,1:T(8,128)}), f32[4096,4,128]{2,0,1:T(8,128)}, u32[]{:S(2)}, u32[]{:S(2)}) async-start(f32[4096,4,128]{2,0,1:T(8,128)} %copy_bitcast_fusion), calls=%async_computation | async-start | bytes 16777216 | tf_op jit(solution)/shard_map/all_to_all | solution.py:21
  21.1 12.9 %gather_fusion = f32[2048,512]{1,0:T(8,128)} fusion(f32[4096,512]{1,0:T(8,128)} %param.8, s32[2048]{0:T(1024)S(1)} %fusion.5), kind=kCustom, calls=%fused_computation | custom fusion | bytes 8396800 | tf_op jit(solution)/shard_map/jit(_take)/gather | solution.py:13
  34.1 3.9 select_select_fusion
  38.1 5.9 %convert_element_type.7 = bf16[4096,512]{1,0:T(8,128)(2,1)} convert(f32[4096,512]{1,0:T(8,128)} %param.8) | non-fusion elementwise | flops 2097152 | bytes 12582912 | tf_op jit(solution)/shard_map/convert_element_type | solution.py:26
  44.0 0.7 fusion.9
  44.6 0.7 fusion.7
  45.4 0.7 fusion.6
  46.1 0.7 fusion.8
  46.8 39.9 %select_select_fusion.1 = f32[2048]{0:T(1024)S(1)} fusion(s32[2048]{0:T(1024)S(1)} %copy-done.4, f32[]{:T(128)} %bitcast.6, f32[]{:T(128)} %bitcast.7, f32[]{:T(128)} %bitcast.8, f32[]{:T(128)} %bitcast.9, f32[]{:T(128)} %bitcast.10, f32[]{:T(128)} %bitcast.11, f32[]{:T(128)} %bitcast.12, f32[]{:T(128)} %bitcast.13, f32[]{:T(128)} %bitcast.14, f32[]{:T(128)} %bitcast.15, ...), kind=kLoop, calls=%fused_computation.15 | loop fusion | flops 272384 | bytes 16640 | tf_op jit(solution)/shard_map/jit(_take)/select_n | solution.py:27
  86.8 8.9 %gather_fusion.1 = f32[2048,512]{1,0:T(8,128)} fusion(f32[822,512]{1,0:T(8,128)S(1)} %copy-done, s32[2048]{0:T(1024)S(1)} %fusion.4), kind=kCustom, calls=%fused_computation.1 | custom fusion | bytes 8396800 | tf_op jit(solution)/shard_map/jit(_take)/gather | solution.py:25
  95.7 223.5 %all-reduce.3.cloned.1.call-done = f32[2048,512]{1,0:T(8,128)} async-done(((f32[2048,512]{1,0:T(8,128)}), f32[2048,512]{1,0:T(8,128)}) %all-reduce.3.cloned.1.call-update) | async-done | bytes 4194320 | tf_op jit(solution)/shard_map/psum | solution.py:24
  319.2 4.7 %multiply_convert_fusion = bf16[2048,512]{1,0:T(8,128)(2,1)} fusion(f32[2048,512]{1,0:T(8,128)} %all-reduce.3.cloned.1.call-done, f32[2048,512]{1,0:T(8,128)} %gather_fusion.1, pred[2048]{0:T(1024)(128)(4,1)S(1)} %compare_and_fusion), kind=kLoop, calls=%fused_computation.10 | loop fusion | flops 3145728 | bytes 10487808 | tf_op jit(solution)/shard_map/convert_element_type | solution.py:25
  323.9 22.9 %while.10 = (s32[]{:T(128)}, f32[4,512]{1,0:T(4,128)S(1)}, bf16[4,512,512]{2,1,0:T(8,128)(2,1)}, bf16[4096,512]{1,0:T(8,128)(2,1)}, f32[4,512]{1,0:T(4,128)S(1)}, /*index=5*/s32[]{:T(128)}, s32[]{:T(128)}) while((s32[]{:T(128)}, f32[4,512]{1,0:T(4,128)S(1)}, bf16[4,512,512]{2,1,0:T(8,128)(2,1)}, bf16[4096,512]{1,0:T(8,128)(2,1)}, ...), condition=%wide.region_3.4_spmd, body=%wide.region_1.3_spmd.sunk | while | flops 2160066560 | bytes 4735073 | solution.py:38
  323.9 5.6 %fusion.17 = f32[512]{0:T(512)S(1)} fusion(bf16[4096,512]{1,0:T(8,128)(2,1)} %get-tuple-element.154, f32[512]{0:T(512)S(1)} %bitcast.91, bf16[4,512,512]{2,1,0:T(8,128)(2,1)} %get-tuple-element.153, s32[]{:T(128)S(6)} %copy.17), kind=kOutput, calls=%fused_computation.3.clone.1 | convolution fusion | flops 2160066048 | bytes 4722692 | tf_op jit(solution)/shard_map/while/body/eval_jaxpr/dot_general | solution.py:34
  329.6 0.1 dynamic_update_slice.5
  329.6 5.6 %fusion.17 = f32[512]{0:T(512)S(1)} fusion(bf16[4096,512]{1,0:T(8,128)(2,1)} %get-tuple-element.154, f32[512]{0:T(512)S(1)} %bitcast.91, bf16[4,512,512]{2,1,0:T(8,128)(2,1)} %get-tuple-element.153, s32[]{:T(128)S(6)} %copy.17), kind=kOutput, calls=%fused_computation.3.clone.1 | convolution fusion | flops 2160066048 | bytes 4722692 | tf_op jit(solution)/shard_map/while/body/eval_jaxpr/dot_general | solution.py:34
  335.3 0.1 dynamic_update_slice.5
  335.4 5.6 %fusion.17 = f32[512]{0:T(512)S(1)} fusion(bf16[4096,512]{1,0:T(8,128)(2,1)} %get-tuple-element.154, f32[512]{0:T(512)S(1)} %bitcast.91, bf16[4,512,512]{2,1,0:T(8,128)(2,1)} %get-tuple-element.153, s32[]{:T(128)S(6)} %copy.17), kind=kOutput, calls=%fused_computation.3.clone.1 | convolution fusion | flops 2160066048 | bytes 4722692 | tf_op jit(solution)/shard_map/while/body/eval_jaxpr/dot_general | solution.py:34
  341.0 0.1 dynamic_update_slice.5
  341.1 5.6 %fusion.17 = f32[512]{0:T(512)S(1)} fusion(bf16[4096,512]{1,0:T(8,128)(2,1)} %get-tuple-element.154, f32[512]{0:T(512)S(1)} %bitcast.91, bf16[4,512,512]{2,1,0:T(8,128)(2,1)} %get-tuple-element.153, s32[]{:T(128)S(6)} %copy.17), kind=kOutput, calls=%fused_computation.3.clone.1 | convolution fusion | flops 2160066048 | bytes 4722692 | tf_op jit(solution)/shard_map/while/body/eval_jaxpr/dot_general | solution.py:34
  346.8 39.4 %all-reduce = f32[2048]{0:T(1024)S(1)} all-reduce(f32[2048]{0:T(1024)S(1)} %bitcast.92), channel_id=2, replica_groups=mesh['rows'=8,'dim'=4] {'rows','dim'}, use_global_device_ids=true, to_apply=%region_4.5.clone | all-reduce | flops 2048 | bytes 16384
  386.3 0.6 dynamic-slice
  386.9 5.9 %copy.22 = f32[16384,128]{1,0:T(8,128)} copy(f32[16384,128]{1,0:T(8,128)} %bitcast.4) | data formatting | bytes 16777216
  (29 shorter events, 0.2 us)
Async XLA Ops:
  7.2 79.7 %copy-start = (f32[822,512]{1,0:T(8,128)S(1)}, f32[822,512]{1,0:T(8,128)}, u32[]{:S(2)}) copy-start(f32[822,512]{1,0:T(8,128)} %param.9) | copy-start | bytes 5050372
  14.6 6.5 %copy-start.3 = (s32[2048]{0:T(1024)S(1)}, s32[2048]{0:T(1024)}, u32[]{:S(2)}) copy-start(s32[2048]{0:T(1024)} %param.11) | copy-start | bytes 24580
  14.6 372.2 %all-to-all-start = ((f32[4096,4,128]{2,0,1:T(8,128)}), f32[4096,4,128]{2,0,1:T(8,128)}, u32[]{:S(2)}, u32[]{:S(2)}) async-start(f32[4096,4,128]{2,0,1:T(8,128)} %copy_bitcast_fusion), calls=%async_computation | async-start | bytes 16777216 | tf_op jit(solution)/shard_map/all_to_all | solution.py:21
  21.1 298.1 %all-reduce.3.cloned.1.call-start = ((), (), s32[]{:S(2)}) async-start(), calls=%async_computation.1 | async-start | bytes 8388608 | tf_op jit(solution)/shard_map/psum | solution.py:24
  38.0 5.9 %copy-start.1 = (f32[64]{0:T(128)S(1)}, f32[64]{0:T(128)}, u32[]{:S(2)}) copy-start(f32[64]{0:T(128)} %param.10) | copy-start | bytes 772
  38.0 8.8 %copy-start.4 = (s32[2048]{0:T(1024)S(1)}, s32[2048]{0:T(1024)}, u32[]{:S(2)}) copy-start(s32[2048]{0:T(1024)} %param.13) | copy-start | bytes 24580
  38.1 48.7 %copy-start.2 = (s32[2048]{0:T(1024)S(1)}, s32[2048]{0:T(1024)}, u32[]{:S(2)}) copy-start(s32[2048]{0:T(1024)} %param.12) | copy-start | bytes 24580
Sparse Core Ops, SparseCore 0:
  38.1 280.9 all-reduce.2
where the time goes:
time: 401 us; the launch traced here: 400 us
  waiting for transfers between devices  223 us (56%)
  other arithmetic  54.6 us (14%)
  blocking collectives  39.4 us (10%)
  local copies, waits for them, and re-layouts  38.8 us (10%)
  matrix products  22.6 us (6%)
  between operations  14.2 us (4%)
  starting transfers between devices  6.48 us (2%)
    psum x1, waiting for transfers between devices, shards(): head_vecs = lax.psum(partial_value, ('rows', 'dim'))  223 us
    select_n x1, other arithmetic, shards(): level = jnp.take(thresholds, thr_idx)  39.9 us
    unnamed x1, blocking collectives  39.4 us
    dot_general x4, matrix products, score_block(): score = jnp.dot(rows_q, ent_low.T, preferred_element_type=jnp.float32)  22.6 us
    gather x1, local copies, waits for them, and re-layouts, pick_rows(): picked = jnp.take(table, jnp.clip(local, 0, count - 1), axis=0)  12.9 us
    gather x1, local copies, waits for them, and re-layouts, shards(): jnp.take(relations, rel_ids, axis=0)  8.85 us
  transfers between devices with their start and end apart: 2, of which 1 were waited for; matrix products, arithmetic and copies ran while one was open for 26% of the time, Pallas kernels for 0%

commit v1 on v0

--- a/solution.py
+++ b/solution.py
@@ -21,7 +21,7 @@
     serving = lax.all_to_all(entity_table, "dim", split_axis=1, concat_axis=0, tiled=True)
     start = (lax.axis_index("rows") * lax.axis_size("dim") + lax.axis_index("dim")) * local_rows
     partial_value = pick_rows(entity_table, head_ids, start)
-    head_vecs = lax.psum(partial_value, ("rows", "dim"))
+    head_vecs = lax.psum(lax.psum(partial_value, "dim"), "rows")
     query = (head_vecs * jnp.take(relations, rel_ids, axis=0)).astype(jnp.bfloat16)
     ent_low = entity_table.astype(jnp.bfloat16)
     level = jnp.take(thresholds, thr_idx)

time: 401 us -> 505 us (1.26)
  waiting for transfers between devices: 223 us -> 327 us
    psum x1 -> x2, waiting for transfers between devices: 223 us -> 327 us  [shards(): head_vecs = lax.psum(lax.psum(partial_value, 'dim'), 'rows')]
  transfers between devices with their start and end apart: 2 -> 3, of which waited for: 1 -> 2; matrix products, arithmetic and copies ran while one was open for 26% -> 18% of each run, Pallas kernels for 0% -> 0%
where the time goes in v1:
time: 505 us; the launch traced here: 504 us
  waiting for transfers between devices  327 us (65%)
  other arithmetic  55.9 us (11%)
  blocking collectives  39.4 us (8%)
  local copies, waits for them, and re-layouts  38.7 us (8%)
  matrix products  22.6 us (4%)
  between operations  14.2 us (3%)
  starting transfers between devices  6.51 us (1%)
    psum x2, waiting for transfers between devices, shards(): head_vecs = lax.psum(lax.psum(partial_value, 'dim'), 'rows')  327 us
    select_n x1, other arithmetic, shards(): level = jnp.take(thresholds, thr_idx)  39.8 us
    unnamed x1, blocking collectives  39.4 us
    dot_general x4, matrix products, score_block(): score = jnp.dot(rows_q, ent_low.T, preferred_element_type=jnp.float32)  22.6 us
    gather x1, local copies, waits for them, and re-layouts, pick_rows(): picked = jnp.take(table, jnp.clip(local, 0, count - 1), axis=0)  12.9 us
  transfers between devices with their start and end apart: 3, of which 2 were waited for; matrix products, arithmetic and copies ran while one was open for 18% of the time, Pallas kernels for 0%

profile of v1, /device:TPU:0, one launch (start us, length us, event | category | flops | bytes accessed | tf_op | source)
XLA Modules:
  0.0 504.2 jit_solution(10360126017225137305)
XLA Ops:
  7.2 0.8 compare_and_fusion.2
  8.1 0.7 fusion.5
  8.8 12.9 %gather_fusion = f32[2048,512]{1,0:T(8,128)} fusion(f32[4096,512]{1,0:T(8,128)} %param.8, s32[2048]{0:T(1024)S(1)} %fusion.5), kind=kCustom, calls=%fused_computation | custom fusion | bytes 8396800 | tf_op jit(solution)/shard_map/jit(_take)/gather | solution.py:13
  21.6 3.9 select_select_fusion
  25.6 7.3 %copy_bitcast_fusion = f32[4096,4,128]{2,0,1:T(8,128)} fusion(f32[4096,512]{1,0:T(8,128)} %param.8), kind=kLoop, calls=%fused_computation.9 | loop fusion | bytes 16777216 | tf_op jit(solution)/shard_map/all_to_all | solution.py:21
  32.9 6.5 %all-to-all-start = ((f32[4096,4,128]{2,0,1:T(8,128)}), f32[4096,4,128]{2,0,1:T(8,128)}, u32[]{:S(2)}, u32[]{:S(2)}) async-start(f32[4096,4,128]{2,0,1:T(8,128)} %copy_bitcast_fusion), calls=%async_computation | async-start | bytes 16777216 | tf_op jit(solution)/shard_map/all_to_all | solution.py:21
  39.4 302.2 %all-reduce.4.cloned.1.call-done = f32[2048,512]{1,0:T(8,128)} async-done(((f32[2048,512]{1,0:T(8,128)}), f32[2048,512]{1,0:T(8,128)}) %all-reduce.4.cloned.1.call-update) | async-done | bytes 4194320 | tf_op jit(solution)/shard_map/psum | solution.py:24
  341.7 5.9 %convert_element_type.7 = bf16[4096,512]{1,0:T(8,128)(2,1)} convert(f32[4096,512]{1,0:T(8,128)} %param.8) | non-fusion elementwise | flops 2097152 | bytes 12582912 | tf_op jit(solution)/shard_map/convert_element_type | solution.py:26
  347.6 0.7 fusion.9
  348.2 0.7 fusion.7
  348.9 0.7 fusion.6
  349.7 0.7 fusion.8
  350.4 39.8 %select_select_fusion.1 = f32[2048]{0:T(1024)S(1)} fusion(s32[2048]{0:T(1024)S(1)} %copy-done.3, f32[]{:T(128)} %bitcast.6, f32[]{:T(128)} %bitcast.7, f32[]{:T(128)} %bitcast.8, f32[]{:T(128)} %bitcast.9, f32[]{:T(128)} %bitcast.10, f32[]{:T(128)} %bitcast.11, f32[]{:T(128)} %bitcast.12, f32[]{:T(128)} %bitcast.13, f32[]{:T(128)} %bitcast.14, f32[]{:T(128)} %bitcast.15, ...), kind=kLoop, calls=%fused_computation.15 | loop fusion | flops 272384 | bytes 16640 | tf_op jit(solution)/shard_map/jit(_take)/select_n | solution.py:27
  390.2 9.0 %gather_fusion.1 = f32[2048,512]{1,0:T(8,128)} fusion(f32[822,512]{1,0:T(8,128)S(1)} %copy-done, s32[2048]{0:T(1024)S(1)} %fusion.4), kind=kCustom, calls=%fused_computation.1 | custom fusion | bytes 8396800 | tf_op jit(solution)/shard_map/jit(_take)/gather | solution.py:25
  399.2 24.7 %all-reduce.6.cloned.1.call-done = f32[2048,512]{1,0:T(8,128)} async-done(((f32[2048,512]{1,0:T(8,128)}), f32[2048,512]{1,0:T(8,128)}) %all-reduce.6.cloned.1.call-update) | async-done | bytes 4194320 | tf_op jit(solution)/shard_map/psum | solution.py:24
  423.8 4.7 multiply_convert_fusion
  428.6 22.9 %while.10 = (s32[]{:T(128)}, f32[4,512]{1,0:T(4,128)S(1)}, bf16[4,512,512]{2,1,0:T(8,128)(2,1)}, bf16[4096,512]{1,0:T(8,128)(2,1)}, f32[4,512]{1,0:T(4,128)S(1)}, /*index=5*/s32[]{:T(128)}, s32[]{:T(128)}) while((s32[]{:T(128)}, f32[4,512]{1,0:T(4,128)S(1)}, bf16[4,512,512]{2,1,0:T(8,128)(2,1)}, bf16[4096,512]{1,0:T(8,128)(2,1)}, ...), condition=%wide.region_4.5_spmd, body=%wide.region_2.4_spmd.sunk | while | flops 2160066560 | bytes 4735073 | solution.py:38
  428.6 5.6 %fusion.17 = f32[512]{0:T(512)S(1)} fusion(bf16[4096,512]{1,0:T(8,128)(2,1)} %get-tuple-element.154, f32[512]{0:T(512)S(1)} %bitcast.91, bf16[4,512,512]{2,1,0:T(8,128)(2,1)} %get-tuple-element.153, s32[]{:T(128)S(6)} %copy.18), kind=kOutput, calls=%fused_computation.3.clone.1 | convolution fusion | flops 2160066048 | bytes 4722692 | tf_op jit(solution)/shard_map/while/body/eval_jaxpr/dot_general | solution.py:34
  434.3 5.6 %fusion.17 = f32[512]{0:T(512)S(1)} fusion(bf16[4096,512]{1,0:T(8,128)(2,1)} %get-tuple-element.154, f32[512]{0:T(512)S(1)} %bitcast.91, bf16[4,512,512]{2,1,0:T(8,128)(2,1)} %get-tuple-element.153, s32[]{:T(128)S(6)} %copy.18), kind=kOutput, calls=%fused_computation.3.clone.1 | convolution fusion | flops 2160066048 | bytes 4722692 | tf_op jit(solution)/shard_map/while/body/eval_jaxpr/dot_general | solution.py:34
  440.0 5.6 %fusion.17 = f32[512]{0:T(512)S(1)} fusion(bf16[4096,512]{1,0:T(8,128)(2,1)} %get-tuple-element.154, f32[512]{0:T(512)S(1)} %bitcast.91, bf16[4,512,512]{2,1,0:T(8,128)(2,1)} %get-tuple-element.153, s32[]{:T(128)S(6)} %copy.18), kind=kOutput, calls=%fused_computation.3.clone.1 | convolution fusion | flops 2160066048 | bytes 4722692 | tf_op jit(solution)/shard_map/while/body/eval_jaxpr/dot_general | solution.py:34
  445.8 5.6 %fusion.17 = f32[512]{0:T(512)S(1)} fusion(bf16[4096,512]{1,0:T(8,128)(2,1)} %get-tuple-element.154, f32[512]{0:T(512)S(1)} %bitcast.91, bf16[4,512,512]{2,1,0:T(8,128)(2,1)} %get-tuple-element.153, s32[]{:T(128)S(6)} %copy.18), kind=kOutput, calls=%fused_computation.3.clone.1 | convolution fusion | flops 2160066048 | bytes 4722692 | tf_op jit(solution)/shard_map/while/body/eval_jaxpr/dot_general | solution.py:34
  451.5 39.4 %all-reduce = f32[2048]{0:T(1024)S(1)} all-reduce(f32[2048]{0:T(1024)S(1)} %bitcast.92), channel_id=2, replica_groups=mesh['rows'=8,'dim'=4] {'rows','dim'}, use_global_device_ids=true, to_apply=%region_5.6.clone | all-reduce | flops 2048 | bytes 16384
  490.9 0.6 dynamic-slice
  491.5 5.9 %copy.23 = f32[16384,128]{1,0:T(8,128)} copy(f32[16384,128]{1,0:T(8,128)} %bitcast.4) | data formatting | bytes 16777216
  (30 shorter events, 0.4 us)
Async XLA Ops:
  7.2 383.0 %copy-start = (f32[822,512]{1,0:T(8,128)S(1)}, f32[822,512]{1,0:T(8,128)}, u32[]{:S(2)}) copy-start(f32[822,512]{1,0:T(8,128)} %param.9) | copy-start | bytes 5050372
  7.2 334.4 %all-reduce.4.cloned.1.call-start = ((), (), s32[]{:S(2)}) async-start(), calls=%async_computation.1 | async-start | bytes 8388608 | tf_op jit(solution)/shard_map/psum | solution.py:24
  32.9 458.6 %all-to-all-start = ((f32[4096,4,128]{2,0,1:T(8,128)}), f32[4096,4,128]{2,0,1:T(8,128)}, u32[]{:S(2)}, u32[]{:S(2)}) async-start(f32[4096,4,128]{2,0,1:T(8,128)} %copy_bitcast_fusion), calls=%async_computation | async-start | bytes 16777216 | tf_op jit(solution)/shard_map/all_to_all | solution.py:21
  39.4 384.5 %all-reduce.6.cloned.1.call-start = ((), (), s32[]{:S(2)}) async-start(), calls=%async_computation.2 | async-start | bytes 8388608 | tf_op jit(solution)/shard_map/psum | solution.py:24
  341.6 5.9 %copy-start.1 = (f32[64]{0:T(128)S(1)}, f32[64]{0:T(128)}, u32[]{:S(2)}) copy-start(f32[64]{0:T(128)} %param.10) | copy-start | bytes 772
  341.6 8.7 %copy-start.3 = (s32[2048]{0:T(1024)S(1)}, s32[2048]{0:T(1024)}, u32[]{:S(2)}) copy-start(s32[2048]{0:T(1024)} %param.13) | copy-start | bytes 24580
  341.7 48.5 %copy-start.2 = (s32[2048]{0:T(1024)S(1)}, s32[2048]{0:T(1024)}, u32[]{:S(2)}) copy-start(s32[2048]{0:T(1024)} %param.12) | copy-start | bytes 24580
Sparse Core Ops, SparseCore 0:
  25.7 315.8 all-reduce.3
  344.9 78.9 all-reduce.5
